TPU v7x, 256 devices: a whole 4x4x8 slice. The times are simulated.
256 devices in a mesh: dp: 64 (over z, x, core), tensor: 4 (over y).
Axes of the slice: x: 4, y: 4, z: 8, core: 2. Of those that a mesh axis runs over, the one named last changes fastest.
Arguments:
- master_old: float32 [3072, 36864], P('dp', 'tensor'), may hold values from -6 to 6
- moment1_old: float32 [3072, 36864], P('dp', 'tensor'), may hold values from -4 to 4
- moment2_old: float32 [3072, 36864], P('dp', 'tensor'), may hold values from 0.0001 to 1
- grad: bfloat16 [3072, 36864], P('dp', 'tensor'), may hold values from -28 to 28
- send_slots: int32 [64, 1728], P('dp'), may hold values from 0 to 1727, each once within a row
- recv_slots: int32 [64, 1728], P('dp'), may hold values from 0 to 1727, each once within a row
Outputs:
- master_new: float32 [3072, 36864], P('dp', 'tensor')
- moment1_new: float32 [3072, 36864], P('dp', 'tensor')
- moment2_new: float32 [3072, 36864], P('dp', 'tensor')
Inputs may be any that keep to these rules, and one draw needn't show every extreme that they name: `send_slots`: each row is a permutation of 0 to 1727; entry [i, j * 27 + q] is the old slot of the q-th block that device i of dp sends to device j. `recv_slots`: each row is a permutation of 0 to 1727; entry [j, i * 27 + q] is the new slot on device j of the q-th block from device i.
All inputs are finite; a program needn't handle non-finite values.
Results may differ from a plain program's by a relative error of at most 0.0003.
Values sent between devices are 32-bit elements; how exact they have to be, the bound alone decides.
No kernel may reach another device: no remote copies, remote signals or barrier semaphores. Data moves between devices by JAX's collectives and lax.ppermute only.
A program may use at most 64 MiB of HBM per device.

v0:
```python
import functools

import jax
import jax.numpy as jnp
from jax import lax
from jax.sharding import Mesh
from jax.sharding import PartitionSpec as P

ROWS = 3072
FF = 36864
SEGW = 128
DP = ("dp_0", "dp_1", "dp_2")
DP_TENSOR = ("dp_0", "dp_1", "dp_2", "tensor")


beta_one = 0.9
beta_two = 0.95
correct_one = 0.6513215599
correct_two = 0.4012630608
adam_eps = 1e-08
learning_rate = 0.01
weight_decay = 0.1
clip_ratio = 0.75


def one_axis_at_a_time(value, axes):
    return functools.reduce(lax.psum, axes, value)


def swapped(block, axis, apart):
    count = lax.axis_size(axis)
    route = []
    for low in range(count):
        high = low | 1 << apart
        if high != low and high < count:
            route += [(low, high), (high, low)]
    return lax.ppermute(block, axis, route)


def per_device(master_old, moment1_old, moment2_old, grad, send_slots, recv_slots):
    rows_here, columns = master_old.shape
    half_width = columns // 2
    segments = half_width // SEGW
    blocks = rows_here * segments
    devices = lax.axis_size(DP)
    per_peer = blocks // devices
    is_even = lax.axis_index("tensor") % 2 == 0
    wide = grad.astype(jnp.float32)
    sum_squares = one_axis_at_a_time(jnp.sum(wide * wide), DP_TENSOR)
    stacked = jnp.stack([master_old, moment1_old, moment2_old], 0)
    tiled = (
        stacked.reshape(3, rows_here, 2, segments, SEGW)
        .transpose(0, 1, 3, 2, 4)
        .reshape(3, blocks, 2, SEGW)
    )
    own_send = send_slots[0]
    own_recv = recv_slots[0]
    outgoing = jnp.take(tiled, own_send, axis=1).reshape(3, devices, per_peer, 2, SEGW)
    arrived = lax.all_to_all(outgoing, DP, split_axis=1, concat_axis=1, tiled=True).reshape(
        3, blocks, 2, SEGW
    )
    inverse = jnp.zeros((blocks,), jnp.int32).at[own_recv].set(jnp.arange(blocks, dtype=jnp.int32))
    tiles = jnp.take(arrived, inverse, axis=1)
    first = tiles[..., 0, :]
    second = tiles[..., 1, :]
    kept = jnp.where(is_even, first, second)
    outgoing = jnp.where(is_even, second, first)
    arrived = swapped(outgoing, "tensor", 0)
    moved = jnp.where(is_even, jnp.stack([kept, arrived], -2), jnp.stack([arrived, kept], -2))
    placed = (
        moved.reshape(3, rows_here, segments, 2, SEGW)
        .transpose(0, 1, 3, 2, 4)
        .reshape(3, rows_here, columns)
    )
    new_master = placed[0]
    new_first = placed[1]
    new_second = placed[2]
    limit = clip_ratio * jnp.sqrt(jnp.float32(ROWS * FF))
    clip_scale = jnp.minimum(1.0, limit / jnp.sqrt(sum_squares + 1e-06))
    scaled = clip_scale * wide
    moment1 = beta_one * new_first + (1.0 - beta_one) * scaled
    moment2 = beta_two * new_second + (1.0 - beta_two) * scaled * scaled
    update = moment1 / correct_one / (jnp.sqrt(moment2 / correct_two) + adam_eps)
    master = new_master - learning_rate * (update + weight_decay * new_master)
    return (master, moment1, moment2)


def solution(mesh):
    split = Mesh(
        mesh.devices.reshape(8, 4, 2, mesh.shape["tensor"]), ("dp_0", "dp_1", "dp_2", "tensor")
    )
    return jax.shard_map(
        per_device,
        mesh=split,
        in_specs=(
            P(DP, "tensor"),
            P(DP, "tensor"),
            P(DP, "tensor"),
            P(DP, "tensor"),
            P(DP, None),
            P(DP, None),
        ),
        out_specs=(P(DP, "tensor"), P(DP, "tensor"), P(DP, "tensor")),
        check_vma=False,
    )
```

profile of v0, /device:TPU:1, one launch (start us, length us, event | category | flops | bytes accessed | tf_op | source)
XLA Modules:
  0.0 299.1 jit_solution(16645460600656540258)
XLA Ops:
  3.0 2.8 stack.27
  5.7 2.7 stack.26
  8.5 2.6 maximum_bitcast_fusion
  11.1 5.0 %copy.37 = f32[3,48,36,2,128]{4,3,2,1,0:T(2,128)} copy(f32[3,48,36,2,128]{4,2,3,1,0:T(8,128)S(1)} %maximum_bitcast_fusion) | data formatting | bytes 10616832 | tf_op jit(solution)/shard_map/transpose | solution.py:53
  16.1 15.3 %gather_fusion = f32[1728,3,2,128]{3,2,1,0:T(2,128)} fusion(f32[3,1728,2,128]{3,2,1,0:T(2,128)} %bitcast.18, s32[2048]{0:T(1024)S(1)} %pad_clamp_fusion.1), kind=kCustom, calls=%fused_computation.clone | custom fusion | bytes 10623744 | tf_op jit(solution)/shard_map/jit(_take)/gather | solution.py:58
  31.5 8.1 %broadcast_select_fusion = f32[1728,3,2,128]{3,2,1,0:T(2,128)S(1)} fusion(f32[1728,3,2,128]{3,2,1,0:T(2,128)} %gather_fusion, pred[1728]{0:T(1024)(128)(4,1)S(1)} %compare_and_fusion.1), kind=kLoop, calls=%fused_computation.7 | loop fusion | flops 1327104 | bytes 10618560 | tf_op jit(solution)/shard_map/jit(_take)/select_n | solution.py:58
  39.5 4.2 %copy.38 = f32[3,64,27,2,128]{4,3,2,0,1:T(2,128)} copy(f32[3,64,27,2,128]{4,3,0,2,1:T(2,128)S(1)} %bitcast.19) | data formatting | bytes 10616832 | tf_op jit(solution)/shard_map/reshape | solution.py:58
  43.7 13.5 %all-to-all-start = ((f32[3,64,27,2,128]{4,3,2,0,1:T(2,128)}), f32[3,64,27,2,128]{4,3,2,0,1:T(2,128)}, u32[]{:S(2)}, u32[]{:S(2)}) async-start(f32[3,64,27,2,128]{4,3,2,0,1:T(2,128)} %copy.38), calls=%async_computation | async-start | bytes 10616832 | tf_op jit(solution)/shard_map/all_to_all | solution.py:59
  57.2 8.8 %scatter_custom_fusion = s32[1728]{0:T(1024)S(1)} fusion(s32[1728]{0:T(1024)S(1)} %fusion.5, s32[1728]{0:T(1024)S(1)} %iota.3, s32[]{:T(128)} %constant.26.clone.1), kind=kCustom, calls=%fused_computation.29 | custom fusion | bytes 6916 | tf_op jit(solution)/shard_map/scatter | solution.py:62
  66.1 109.1 %all-to-all-done = f32[3,64,27,2,128]{4,3,2,0,1:T(2,128)} async-done(((f32[3,64,27,2,128]{4,3,2,0,1:T(2,128)}), f32[3,64,27,2,128]{4,3,2,0,1:T(2,128)}, u32[]{:S(2)}, u32[]{:S(2)}) %all-to-all-start) | async-done | bytes 5308448 | tf_op jit(solution)/shard_map/all_to_all | solution.py:59
  175.2 6.7 %copy.39 = f32[3,64,27,2,128]{4,3,2,1,0:T(2,128)} copy(f32[3,64,27,2,128]{4,3,2,0,1:T(2,128)} %all-to-all-done) | data formatting | bytes 10616832 | tf_op jit(solution)/shard_map/all_to_all | solution.py:59
  181.9 15.4 %gather_fusion.1 = f32[1728,3,2,128]{3,2,1,0:T(2,128)} fusion(f32[3,1728,2,128]{3,2,1,0:T(2,128)} %bitcast.17, s32[2048]{0:T(1024)S(1)} %pad_clamp_fusion), kind=kCustom, calls=%fused_computation.1.clone | custom fusion | bytes 10623744 | tf_op jit(solution)/shard_map/jit(_take)/gather | solution.py:63
  197.2 8.1 %select_bitcast_fusion = f32[3,1728,2,128]{3,2,0,1:T(2,128)S(1)} fusion(f32[1728,3,2,128]{3,2,1,0:T(2,128)} %gather_fusion.1, pred[1728]{0:T(1024)(128)(4,1)S(1)} %compare_and_fusion), kind=kLoop, calls=%fused_computation.6 | loop fusion | flops 1327104 | bytes 10618560 | tf_op jit(solution)/shard_map/jit(_take)/select_n | solution.py:63
  205.3 3.9 %broadcast_select_fusion.2 = (f32[3,1728,1,128]{3,2,0,1:T(1,128)S(1)}, f32[3,1728,1,128]{3,2,0,1:T(1,128)S(1)}) fusion(pred[]{:T(512)S(6)} %eq.5, f32[3,1728,2,128]{3,2,0,1:T(2,128)S(1)} %select_bitcast_fusion), kind=kLoop, calls=%fused_computation.9 | loop fusion | flops 1327104 | bytes 10616833 | tf_op jit(solution)/shard_map/jit(_where)/select_n | solution.py:66
  213.3 13.7 %psum.28 = f32[]{:T(128)} all-reduce(f32[]{:T(128)} %fusion.3), channel_id=1, replica_groups=mesh['dp_0'=8,'dp_1'=4,'dp_2'=2,'tensor'=4] {'dp_0'}, use_global_device_ids=true, to_apply=%region_2.4 | all-reduce | flops 1 | bytes 8 | tf_op jit(solution)/shard_map/psum | solution.py:27
  227.0 9.4 %psum.29 = f32[]{:T(128)} all-reduce(f32[]{:T(128)} %psum.28), channel_id=1, replica_groups=mesh['dp_0'=8,'dp_1'=4,'dp_2'=2,'tensor'=4] {'dp_1'}, use_global_device_ids=true, to_apply=%region_3.5 | all-reduce | flops 1 | bytes 8 | tf_op jit(solution)/shard_map/psum | solution.py:27
  236.4 9.2 %psum.30 = f32[]{:T(128)} all-reduce(f32[]{:T(128)} %psum.29), channel_id=1, replica_groups=mesh['dp_0'=8,'dp_1'=4,'dp_2'=2,'tensor'=4] {'dp_2'}, use_global_device_ids=true, to_apply=%region_4.6 | all-reduce | flops 1 | bytes 8 | tf_op jit(solution)/shard_map/psum | solution.py:27
  245.6 26.5 %psum.31 = f32[]{:T(128)} all-reduce(f32[]{:T(128)} %psum.30), channel_id=1, replica_groups=mesh['dp_0'=8,'dp_1'=4,'dp_2'=2,'tensor'=4] {'tensor'}, use_global_device_ids=true, to_apply=%region_5.7 | all-reduce | flops 1 | bytes 8 | tf_op jit(solution)/shard_map/psum | solution.py:27
  272.7 2.7 copy.40
  277.2 2.5 stack.31
  282.1 2.2 slice_multiply_fusion
  286.3 2.1 copy.47
  289.9 2.1 copy.48
  293.4 5.7 %multiply_subtract_fusion = (f32[48,9216]{1,0:T(8,128)}, f32[48,9216]{1,0:T(8,128)}, f32[48,9216]{1,0:T(8,128)}) fusion(f32[48,9216]{1,0:T(8,128)} %squeeze.15, f32[48,9216]{1,0:T(8,128)} %mul.50, bf16[48,9216]{1,0:T(8,128)(2,1)S(1)} %copy-done.2, f32[]{:T(128)S(6)} %min_shard_map.3, f32[48,9216]{1,0:T(8,128)} %mul.57), kind=kLoop, calls=%fused_computation.20 | loop fusion | flops 6635520 | bytes 11501572 | tf_op jit(solution)/shard_map/sub | solution.py:84
  (29 shorter events, 15.6 us)
Async XLA Ops:
  43.7 13.5 %copy-start.3 = (s32[1,1728]{1,0:T(1,128)S(1)}, s32[1,1728]{1,0:T(1,128)}, u32[]{:S(2)}) copy-start(s32[1,1728]{1,0:T(1,128)} %param.13) | copy-start | bytes 20740
  43.7 131.5 %all-to-all-start = ((f32[3,64,27,2,128]{4,3,2,0,1:T(2,128)}), f32[3,64,27,2,128]{4,3,2,0,1:T(2,128)}, u32[]{:S(2)}, u32[]{:S(2)}) async-start(f32[3,64,27,2,128]{4,3,2,0,1:T(2,128)} %copy.38), calls=%async_computation | async-start | bytes 10616832 | tf_op jit(solution)/shard_map/all_to_all | solution.py:59
  209.2 3.0 %copy-start.1 = (bf16[48,9216]{1,0:T(8,128)(2,1)S(1)}, bf16[48,9216]{1,0:T(8,128)(2,1)}, u32[]{:S(2)}) copy-start(bf16[48,9216]{1,0:T(8,128)(2,1)} %param.11) | copy-start | bytes 2654212
  210.9 66.3 %collective-permute-start = (f32[3,1728,128]{2,1,0:T(8,128)}, f32[3,1728,128]{2,1,0:T(8,128)}, u32[]{:S(2)}, u32[]{:S(2)}) collective-permute-start(f32[3,1728,128]{2,1,0:T(8,128)} %bitcast.16), channel_id=1, source_target_pairs={{0,1},{1,0},{2,3},{3,2},{4,5},{5,4},{6,7},{7,6},{8,9},{9,8},{10,11... | collective-permute-start | bytes 7962632 | tf_op jit(solution)/shard_map/ppermute | solution.py:37
  279.7 1.8 copy-start
  291.9 1.5 copy-start.2
where the time goes:
time: 304 us; the launch traced here: 299 us
  waiting for transfers between devices  109 us (36%)
  local copies, waits for them, and re-layouts  81.9 us (27%)
  blocking collectives  58.8 us (19%)
  other arithmetic  33 us (11%)
  starting transfers between devices  14.8 us (5%)
    all_to_all x1, waiting for transfers between devices, per_device(): lax.all_to_all(outgoing, DP, split_axis=1, concat_axis=1, tiled=True)  109 us
    psum x4, blocking collectives, one_axis_at_a_time(): return functools.reduce(lax.psum, axes, value)  58.8 us
    gather x1, local copies, waits for them, and re-layouts, per_device(): tiles = jnp.take(arrived, inverse, axis=1)  15.4 us
    gather x1, local copies, waits for them, and re-layouts, per_device(): jnp.take(tiled, own_send, axis=1).reshape(3, devices, per_peer, 2, SEGW)  15.3 us
    all_to_all x1, starting transfers between devices, per_device(): lax.all_to_all(outgoing, DP, split_axis=1, concat_axis=1, tiled=True)  13.5 us
    scatter x1, local copies, waits for them, and re-layouts, per_device(): jnp.zeros((blocks,), jnp.int32).at[own_recv]  8.77 us
    select_n x2, other arithmetic, per_device(): jnp.take(tiled, own_send, axis=1).reshape(3, devices, per_peer, 2, SEGW)  8.07 us
    select_n x2, other arithmetic, per_device(): tiles = jnp.take(arrived, inverse, axis=1)  8.07 us
  transfers between devices with their start and end apart: 2, of which 1 were waited for; matrix products, arithmetic and copies ran while one was open for 5% of the time, Pallas kernels for 0%

commit v1 on v0

v1 whole, which is shorter than its diff:
```python
import jax
import jax.numpy as jnp
from jax import lax
from jax.experimental import pallas as pl
from jax.experimental.pallas import tpu as pltpu
from jax.sharding import Mesh
from jax.sharding import PartitionSpec as P

SEGW = 128
SUB = 8
DP = ("dp_0", "dp_1", "dp_2")
DP_TENSOR = ("dp_0", "dp_1", "dp_2", "pair", "side")
DP_SIDE = ("dp_0", "dp_1", "dp_2", "side")
PAD = 8

beta_one = 0.9
beta_two = 0.95
correct_one = 0.6513215599
correct_two = 0.4012630608
adam_eps = 1e-08
learning_rate = 0.01
weight_decay = 0.1
clip_ratio = 0.75


def tiled(x, groups, half_rows):
    rows, columns = x.shape
    tiles = x.reshape(groups, SUB, columns // SEGW, SEGW).transpose(0, 2, 1, 3)
    return tiles.reshape(groups, 2, half_rows, SEGW)


def untiled(x, rows, columns):
    groups = rows // SUB
    tiles = x.reshape(groups, columns // SEGW, SUB, SEGW).transpose(0, 2, 1, 3)
    return tiles.reshape(rows, columns)


def in_hbm(x):
    return pltpu.with_memory_space_constraint(x, pltpu.HBM)


def slot_rows(slots, segments, span):
    r = lax.shift_right_logical(slots * (-(-65536 // segments)), 16)
    s = slots - r * segments
    return lax.shift_right_logical(r, 3) * (6 * span) + s * SUB + (r & (SUB - 1))


def pack(xs, slots, devices, per_peer, segments):
    groups, _, half_rows, _ = xs[0].shape
    span = half_rows + PAD
    blocks = devices * per_peer
    message = 3 * per_peer
    at_once = 8
    part = at_once * 2 * message

    def kernel(x0, x1, x2, slot_ref, out, mark, held, sent, slot_v, row_v, row_s, sems, out_sems, row_sems):
        to_vmem = pltpu.make_async_copy(slot_ref, slot_v, row_sems.at[0])
        to_vmem.start()
        copies = []
        for g in range(groups):
            for k in range(2):
                for a, x in enumerate((x0, x1, x2)):
                    at = 6 * g + 3 * k + a
                    copies.append(
                        pltpu.make_async_copy(
                            x.at[g, k], held.at[pl.ds(at * span, half_rows)], sems.at[at]
                        )
                    )
        for c in copies:
            c.start()
        to_vmem.wait()
        row_v[...] = slot_rows(slot_v[...], segments, span)
        to_smem = pltpu.make_async_copy(row_v, row_s, row_sems.at[1])
        to_smem.start()
        mark[...] = jnp.zeros_like(mark)
        to_smem.wait()
        for c in copies:
            c.wait()

        def peer(j, carry):
            for q in range(per_peer):
                row = row_s[0, j * per_peer + q]
                sent[pl.ds(j * 2 * message + q, 6, stride=per_peer), :] = held[
                    pl.ds(row, 6, stride=span), :
                ]
            return carry

        leaving = []
        for n in range(devices // at_once):
            lax.fori_loop(n * at_once, (n + 1) * at_once, peer, 0)
            rows = pl.ds(n * part, part)
            leaving.append(pltpu.make_async_copy(sent.at[rows], out.at[rows], out_sems.at[n]))
            leaving[-1].start()
        for c in leaving:
            c.wait()

    hbm = pl.BlockSpec(memory_space=pltpu.HBM)
    vmem = pl.BlockSpec(memory_space=pltpu.VMEM)
    return pl.pallas_call(
        kernel,
        out_shape=(
            pltpu.HBM((6 * blocks, SEGW), jnp.float32),
            jax.ShapeDtypeStruct((SUB, SEGW), jnp.float32),
        ),
        in_specs=[hbm, hbm, hbm, hbm],
        out_specs=(hbm, vmem),
        scratch_shapes=[
            pltpu.VMEM((6 * groups * span, SEGW), jnp.float32),
            pltpu.VMEM((6 * blocks, SEGW), jnp.float32),
            pltpu.VMEM((1, blocks), jnp.int32),
            pltpu.VMEM((1, blocks), jnp.int32),
            pltpu.SMEM((1, blocks), jnp.int32),
            pltpu.SemaphoreType.DMA((6 * groups,)),
            pltpu.SemaphoreType.DMA((devices // at_once,)),
            pltpu.SemaphoreType.DMA((2,)),
        ],
        compiler_params=pltpu.CompilerParams(vmem_limit_bytes=20 << 20),
        name="pack",
    )(*(in_hbm(x) for x in xs), in_hbm(slots))


def unpack_step(arrived, first_rows, scaled, devices, per_peer, segments):
    groups, _, half_rows, _ = scaled.shape
    span = half_rows + PAD
    blocks = devices * per_peer
    message = 3 * per_peer
    tile = 4 * SUB
    at_once = 8
    part = at_once * 2 * message

    def kernel(in_ref, row_ref, grad_ref, o0, o1, o2, held, came, row_s, sems, in_sems, row_sem):
        to_smem = pltpu.make_async_copy(row_ref, row_s, row_sem)
        to_smem.start()
        coming = []
        for n in range(devices // at_once):
            rows = pl.ds(n * part, part)
            coming.append(pltpu.make_async_copy(in_ref.at[rows], came.at[rows], in_sems.at[n]))
            coming[-1].start()
        to_smem.wait()

        def peer(i, carry):
            for q in range(per_peer):
                row = row_s[0, i * per_peer + q]
                held[pl.ds(row, 6, stride=span), :] = came[
                    pl.ds(i * 2 * message + q, 6, stride=per_peer), :
                ]
            return carry

        for n in range(devices // at_once):
            coming[n].wait()
            lax.fori_loop(n * at_once, (n + 1) * at_once, peer, 0)
        copies = []
        for g in range(groups):
            for k in range(2):
                at = (6 * g + 3 * k) * span

                def update(n, carry, at=at, g=g, k=k):
                    def rows(a):
                        start = pl.multiple_of(at + a * span + n * tile, SUB)
                        return pl.ds(start, tile)

                    scaled_here = grad_ref[g, k, pl.ds(pl.multiple_of(n * tile, SUB), tile), :]
                    old = held[rows(0), :]
                    moment1 = beta_one * held[rows(1), :] + (1.0 - beta_one) * scaled_here
                    moment2 = beta_two * held[rows(2), :] + (1.0 - beta_two) * scaled_here * scaled_here
                    step = moment1 / correct_one / (jnp.sqrt(moment2 / correct_two) + adam_eps)
                    held[rows(0), :] = old - learning_rate * (step + weight_decay * old)
                    held[rows(1), :] = moment1
                    held[rows(2), :] = moment2
                    return carry

                lax.fori_loop(0, half_rows // tile, update, 0)
                for a, o in enumerate((o0, o1, o2)):
                    copies.append(
                        pltpu.make_async_copy(
                            held.at[pl.ds(at + a * span, half_rows)], o.at[g, k], sems.at[6 * g + 3 * k + a]
                        )
                    )
                    copies[-1].start()
        for c in copies:
            c.wait()

    hbm = pl.BlockSpec(memory_space=pltpu.HBM)
    vmem = pl.BlockSpec(memory_space=pltpu.VMEM)
    out = pltpu.HBM(scaled.shape, jnp.float32)
    return pl.pallas_call(
        kernel,
        out_shape=(out, out, out),
        in_specs=[hbm, hbm, vmem],
        out_specs=(hbm, hbm, hbm),
        scratch_shapes=[
            pltpu.VMEM((6 * groups * span, SEGW), jnp.float32),
            pltpu.VMEM((6 * blocks, SEGW), jnp.float32),
            pltpu.SMEM((1, blocks), jnp.int32),
            pltpu.SemaphoreType.DMA((6 * groups,)),
            pltpu.SemaphoreType.DMA((devices // at_once,)),
            pltpu.SemaphoreType.DMA,
        ],
        compiler_params=pltpu.CompilerParams(vmem_limit_bytes=20 << 20),
        name="unpack_step",
    )(in_hbm(arrived), in_hbm(first_rows), scaled)


def sum_over(value, axes):
    for axis in axes:
        count = lax.axis_size(axis)
        apart = 1
        while apart < count:
            route = [(n, n ^ apart) for n in range(count)]
            value = value + lax.ppermute(value, axis, route)
            apart *= 2
    return value


def per_device(total, master_old, moment1_old, moment2_old, grad, send_slots, recv_slots):
    rows, columns = master_old.shape
    segments = columns // 2 // SEGW
    groups, half_rows = rows // SUB, SUB * segments
    devices = lax.axis_size(DP)
    per_peer = rows * segments // devices
    xs = [tiled(x, groups, half_rows) for x in (master_old, moment1_old, moment2_old)]
    packed, mark = pack(xs, send_slots, devices, per_peer, segments)
    outgoing = packed.reshape(2 * devices, 3 * per_peer, 1, SEGW)
    arrived = lax.all_to_all(outgoing, DP_SIDE, split_axis=0, concat_axis=0, tiled=True)
    arrived = arrived.reshape(6 * devices * per_peer, SEGW)

    grad, recv_slots, mark = lax.optimization_barrier((grad, recv_slots, mark))
    first_rows = slot_rows(recv_slots, segments, half_rows + PAD)
    wide = grad.astype(jnp.float32)
    sum_squares = sum_over(jnp.sum(wide * wide).reshape(1, 1), DP_TENSOR)
    limit = clip_ratio * jnp.sqrt(jnp.float32(total))
    clip_scale = jnp.minimum(1.0, limit / jnp.sqrt(sum_squares + 1e-06))
    scaled = tiled(clip_scale * wide, groups, half_rows)
    outs = unpack_step(arrived, first_rows, scaled, devices, per_peer, segments)
    return tuple(untiled(o, rows, columns) for o in outs)


def solution(mesh):
    split = Mesh(mesh.devices.reshape(8, 4, 2, mesh.shape["tensor"] // 2, 2), DP_TENSOR)
    wide_spec = P(DP, ("pair", "side"))

    def whole(master_old, *rest):
        def body(*args):
            return per_device(master_old.size, *args)

        return jax.shard_map(
            body,
            mesh=split,
            in_specs=(wide_spec,) * 4 + (P(DP, None),) * 2,
            out_specs=(wide_spec,) * 3,
            check_vma=False,
        )(master_old, *rest)

    return whole
```

time: 304 us -> 183 us (0.60)
  local copies, waits for them, and re-layouts: 81.9 us -> 0.01 us
  blocking collectives: 58.8 us -> 0 us
  other arithmetic: 33 us -> 1.79 us
  starting transfers between devices: 14.8 us -> 43 us
  Pallas kernels: 0 us -> 14.5 us
  waiting for transfers between devices: 109 us -> 115 us
  between operations: 1.53 us -> 6.5 us
    ppermute x1 -> x8, waiting for transfers between devices: 0.01 us -> 115 us  [sum_over(): value = value + lax.ppermute(value, axis, route)]
    all_to_all x1, waiting for transfers between devices: 109 us -> 0.01 us  [per_device(): lax.all_to_all(outgoing, DP_SIDE, split_axis=0, concat_axis=0, tiled=True)]
    psum x4 -> x0, blocking collectives: 58.8 us -> none  [one_axis_at_a_time(): return functools.reduce(lax.psum, axes, value)]
    gather x2 -> x0, local copies, waits for them, and re-layouts: 30.7 us -> none  [the longest x1 15.4 us: per_device(): tiles = jnp.take(arrived, inverse, axis=1)]
    ppermute x1 -> x8, starting transfers between devices: 1.3 us -> 27.7 us  [sum_over(): value = value + lax.ppermute(value, axis, route)]
    select_n x6 -> x0, other arithmetic: 20.1 us -> none  [the longest x2 8.07 us: per_device(): jnp.take(tiled, own_send, axis=1).reshape(3, devices, per_peer, 2, SEGW)]
    pallas_call x0 -> x2, Pallas kernels: none -> 14.5 us  [the longest x1 7.33 us: pack(): pl.pallas_call(kernel, out_shape=(pltpu.HBM((6 * blocks, SEGW), jnp.float...]
    another operation x6 -> x0, local copies, waits for them, and re-layouts: 11.8 us -> none  [the longest x3 7.1 us: per_device(): stacked = jnp.stack([master_old, moment1_old, moment2_old], 0)]
  transfers between devices with their start and end apart: 2 -> 9, of which waited for: 1 -> 7; matrix products, arithmetic and copies ran while one was open for 5% -> 1% of each run, Pallas kernels for 0% -> 0%
where the time goes in v1:
time: 183 us; the launch traced here: 181 us
  waiting for transfers between devices  115 us (63%)
  starting transfers between devices  43 us (23%)
  Pallas kernels  14.5 us (8%)
  between operations  6.5 us (4%)
    ppermute x8, waiting for transfers between devices, sum_over(): value = value + lax.ppermute(value, axis, route)  115 us
    ppermute x8, starting transfers between devices, sum_over(): value = value + lax.ppermute(value, axis, route)  27.7 us
    all_to_all x1, starting transfers between devices, per_device(): lax.all_to_all(outgoing, DP_SIDE, split_axis=0, concat_axis=0, tiled=True)  15.3 us
    pallas_call x1, Pallas kernels, pack(): pl.pallas_call(kernel, out_shape=(pltpu.HBM((6 * blocks, SEGW), jnp.float...  7.33 us
    pallas_call x1, Pallas kernels, unpack_step(): pl.pallas_call(kernel, out_shape=(out, out, out), in_specs=[hbm, hbm, vme...  7.16 us
  transfers between devices with their start and end apart: 9, of which 7 were waited for; matrix products, arithmetic and copies ran while one was open for 1% of the time, Pallas kernels for 0%

profile of v1, /device:TPU:1, one launch (start us, length us, event | category | flops | bytes accessed | tf_op | source)
XLA Modules:
  0.0 181.1 jit_solution(16557835574424398391)
XLA Ops:
  0.6 7.3 %pack.1 = (f32[10368,128]{1,0:T(8,128)}, f32[8,128]{1,0:T(8,128)}) custom-call(f32[6,2,288,128]{3,2,1,0:T(8,128)} %bitcast.41, f32[6,2,288,128]{3,2,1,0:T(8,128)} %bitcast.42, f32[6,2,288,128]{3,2,1,0:T(8,128)} %bitcast.43, s32[1,1728]{1,0:T(1,128)} %slot_ref.1), custom_call_target="tpu_custom_call" | custom-call | tf_op jit(solution)/shard_map/pack/pallas_call | solution.py:99
  8.0 0.0 copy-start
  8.0 0.0 copy-start.1
  8.0 15.3 %all-to-all-start = ((f32[128,81,1,128]{3,2,1,0:T(1,128)}), f32[128,81,1,128]{3,2,1,0:T(1,128)}, u32[]{:S(2)}, u32[]{:S(2)}) async-start(f32[128,81,1,128]{3,2,1,0:T(1,128)} %bitcast.40), calls=%async_computation | async-start | bytes 10616832 | tf_op jit(solution)/shard_map/all_to_all | solution.py:224
  23.3 1.1 fusion
  24.4 1.4 collective-permute-start
  25.7 0.6 and_add_fusion.row_ref
  26.4 111.4 %collective-permute-done = f32[1,1]{1,0:T(1,128)} collective-permute-done((f32[1,1]{1,0:T(1,128)}, f32[1,1]{1,0:T(1,128)}, u32[]{:S(2)}, u32[]{:S(2)}) %collective-permute-start) | collective-permute-done | bytes 36 | tf_op jit(solution)/shard_map/ppermute | solution.py:210
  139.0 1.6 collective-permute-start.1
  140.6 1.8 collective-permute-done.1
  143.0 6.2 %collective-permute-start.2 = (f32[1,1]{1,0:T(1,128)}, f32[1,1]{1,0:T(1,128)}, u32[]{:S(2)}, u32[]{:S(2)}) collective-permute-start(f32[1,1]{1,0:T(1,128)} %add.36), channel_id=1, source_target_pairs={{0,128},{32,160},{64,192},{96,224},{128,0},{160,32},{192,64},{224,... | collective-permute-start | bytes 20 | tf_op jit(solution)/shard_map/ppermute | solution.py:210
  149.2 0.2 collective-permute-done.2
  150.1 1.7 collective-permute-start.3
  151.8 0.8 collective-permute-done.3
  153.2 3.9 %collective-permute-start.4 = (f32[1,1]{1,0:T(1,128)}, f32[1,1]{1,0:T(1,128)}, u32[]{:S(2)}, u32[]{:S(2)}) collective-permute-start(f32[1,1]{1,0:T(1,128)} %add.38), channel_id=1, source_target_pairs={{0,16},{8,24},{16,0},{24,8},{1,17},{9,25},{17,1},{25,9},{2,18},{10... | collective-permute-start | bytes 20 | tf_op jit(solution)/shard_map/ppermute | solution.py:210
  157.1 0.2 collective-permute-done.4
  157.9 7.5 %collective-permute-start.5 = (f32[1,1]{1,0:T(1,128)}, f32[1,1]{1,0:T(1,128)}, u32[]{:S(2)}, u32[]{:S(2)}) collective-permute-start(f32[1,1]{1,0:T(1,128)} %add.39), channel_id=1, source_target_pairs={{0,4},{4,0},{1,5},{5,1},{2,6},{6,2},{3,7},{7,3},{8,12},{12,8},{9,1... | collective-permute-start | bytes 20 | tf_op jit(solution)/shard_map/ppermute | solution.py:210
  166.0 3.4 %collective-permute-start.6 = (f32[1,1]{1,0:T(1,128)}, f32[1,1]{1,0:T(1,128)}, u32[]{:S(2)}, u32[]{:S(2)}) collective-permute-start(f32[1,1]{1,0:T(1,128)} %add.40), channel_id=1, source_target_pairs={{0,2},{2,0},{1,3},{3,1},{4,6},{6,4},{5,7},{7,5},{8,10},{10,8},{9,1... | collective-permute-start | bytes 20 | tf_op jit(solution)/shard_map/ppermute | solution.py:210
  169.5 0.5 collective-permute-done.6
  170.7 2.0 %collective-permute-start.7 = (f32[1,1]{1,0:T(1,128)}, f32[1,1]{1,0:T(1,128)}, u32[]{:S(2)}, u32[]{:S(2)}) collective-permute-start(f32[1,1]{1,0:T(1,128)} %add.41), channel_id=1, source_target_pairs={{0,1},{1,0},{2,3},{3,2},{4,5},{5,4},{6,7},{7,6},{8,9},{9,8},{10,11... | collective-permute-start | bytes 20 | tf_op jit(solution)/shard_map/ppermute | solution.py:210
  172.6 0.5 collective-permute-done.7
  173.8 0.1 convert_multiply_fusion
  173.9 0.0 all-to-all-done
  173.9 7.2 %unpack_step.1 = (f32[6,2,288,128]{3,2,1,0:T(8,128)}, f32[6,2,288,128]{3,2,1,0:T(8,128)}, f32[6,2,288,128]{3,2,1,0:T(8,128)}) custom-call(f32[10368,128]{1,0:T(8,128)} %bitcast.10.in_ref, s32[1,1728]{1,0:T(1,128)} %and_add_fusion.row_ref, f32[6,2,288,128]{3,2,1,0:T(8,128)S(1)} %bitcast.39), custom_call_target="tpu_custom_call" | custom-call | tf_op jit(solution)/shard_map/unpack_step/pallas_call | solution.py:186
  (3 shorter events, 0.0 us)
Async XLA Ops:
  8.0 15.3 %copy-start = (bf16[48,9216]{1,0:T(8,128)(2,1)S(1)}, bf16[48,9216]{1,0:T(8,128)(2,1)}, u32[]{:S(2)}) copy-start(bf16[48,9216]{1,0:T(8,128)(2,1)} %param.9) | copy-start | bytes 2654212
  8.0 17.8 %copy-start.1 = (s32[1,1728]{1,0:T(1,128)S(1)}, s32[1,1728]{1,0:T(1,128)}, u32[]{:S(2)}) copy-start(s32[1,1728]{1,0:T(1,128)} %param.11) | copy-start | bytes 20740
  8.0 165.9 %all-to-all-start = ((f32[128,81,1,128]{3,2,1,0:T(1,128)}), f32[128,81,1,128]{3,2,1,0:T(1,128)}, u32[]{:S(2)}, u32[]{:S(2)}) async-start(f32[128,81,1,128]{3,2,1,0:T(1,128)} %bitcast.40), calls=%async_computation | async-start | bytes 10616832 | tf_op jit(solution)/shard_map/all_to_all | solution.py:224
  24.4 113.3 %collective-permute-start = (f32[1,1]{1,0:T(1,128)}, f32[1,1]{1,0:T(1,128)}, u32[]{:S(2)}, u32[]{:S(2)}) collective-permute-start(f32[1,1]{1,0:T(1,128)} %bitcast.11), channel_id=1, source_target_pairs={{0,32},{32,0},{64,96},{96,64},{128,160},{160,128},{192,224},{224,1... | collective-permute-start | bytes 20 | tf_op jit(solution)/shard_map/ppermute | solution.py:210
  139.0 3.4 %collective-permute-start.1 = (f32[1,1]{1,0:T(1,128)}, f32[1,1]{1,0:T(1,128)}, u32[]{:S(2)}, u32[]{:S(2)}) collective-permute-start(f32[1,1]{1,0:T(1,128)} %add.35), channel_id=1, source_target_pairs={{0,64},{32,96},{64,0},{96,32},{128,192},{160,224},{192,128},{224,1... | collective-permute-start | bytes 20 | tf_op jit(solution)/shard_map/ppermute | solution.py:210
  143.0 6.4 %collective-permute-start.2 = (f32[1,1]{1,0:T(1,128)}, f32[1,1]{1,0:T(1,128)}, u32[]{:S(2)}, u32[]{:S(2)}) collective-permute-start(f32[1,1]{1,0:T(1,128)} %add.36), channel_id=1, source_target_pairs={{0,128},{32,160},{64,192},{96,224},{128,0},{160,32},{192,64},{224,... | collective-permute-start | bytes 20 | tf_op jit(solution)/shard_map/ppermute | solution.py:210
  150.1 2.5 %collective-permute-start.3 = (f32[1,1]{1,0:T(1,128)}, f32[1,1]{1,0:T(1,128)}, u32[]{:S(2)}, u32[]{:S(2)}) collective-permute-start(f32[1,1]{1,0:T(1,128)} %add.37), channel_id=1, source_target_pairs={{0,8},{8,0},{16,24},{24,16},{1,9},{9,1},{17,25},{25,17},{2,10},{10... | collective-permute-start | bytes 20 | tf_op jit(solution)/shard_map/ppermute | solution.py:210
  153.2 4.1 %collective-permute-start.4 = (f32[1,1]{1,0:T(1,128)}, f32[1,1]{1,0:T(1,128)}, u32[]{:S(2)}, u32[]{:S(2)}) collective-permute-start(f32[1,1]{1,0:T(1,128)} %add.38), channel_id=1, source_target_pairs={{0,16},{8,24},{16,0},{24,8},{1,17},{9,25},{17,1},{25,9},{2,18},{10... | collective-permute-start | bytes 20 | tf_op jit(solution)/shard_map/ppermute | solution.py:210
  157.9 7.5 %collective-permute-start.5 = (f32[1,1]{1,0:T(1,128)}, f32[1,1]{1,0:T(1,128)}, u32[]{:S(2)}, u32[]{:S(2)}) collective-permute-start(f32[1,1]{1,0:T(1,128)} %add.39), channel_id=1, source_target_pairs={{0,4},{4,0},{1,5},{5,1},{2,6},{6,2},{3,7},{7,3},{8,12},{12,8},{9,1... | collective-permute-start | bytes 20 | tf_op jit(solution)/shard_map/ppermute | solution.py:210
  166.0 4.0 %collective-permute-start.6 = (f32[1,1]{1,0:T(1,128)}, f32[1,1]{1,0:T(1,128)}, u32[]{:S(2)}, u32[]{:S(2)}) collective-permute-start(f32[1,1]{1,0:T(1,128)} %add.40), channel_id=1, source_target_pairs={{0,2},{2,0},{1,3},{3,1},{4,6},{6,4},{5,7},{7,5},{8,10},{10,8},{9,1... | collective-permute-start | bytes 20 | tf_op jit(solution)/shard_map/ppermute | solution.py:210
  170.7 2.5 %collective-permute-start.7 = (f32[1,1]{1,0:T(1,128)}, f32[1,1]{1,0:T(1,128)}, u32[]{:S(2)}, u32[]{:S(2)}) collective-permute-start(f32[1,1]{1,0:T(1,128)} %add.41), channel_id=1, source_target_pairs={{0,1},{1,0},{2,3},{3,2},{4,5},{5,4},{6,7},{7,6},{8,9},{9,8},{10,11... | collective-permute-start | bytes 20 | tf_op jit(solution)/shard_map/ppermute | solution.py:210

commit v2 on v1

--- a/solution.py
+++ b/solution.py
@@ -1,3 +1,5 @@
+import math
+
 import jax
 import jax.numpy as jnp
 from jax import lax
@@ -45,15 +47,16 @@
     return lax.shift_right_logical(r, 3) * (6 * span) + s * SUB + (r & (SUB - 1))
 
 
-def pack(xs, slots, devices, per_peer, segments):
+def pack(xs, slots, side, devices, per_peer, segments):
     groups, _, half_rows, _ = xs[0].shape
     span = half_rows + PAD
     blocks = devices * per_peer
-    message = 3 * per_peer
+    message = 3 * per_peer + 1
+    both = 2 * message
     at_once = 8
-    part = at_once * 2 * message
-
-    def kernel(x0, x1, x2, slot_ref, out, mark, held, sent, slot_v, row_v, row_s, sems, out_sems, row_sems):
+    part = at_once * both
+
+    def kernel(side_ref, x0, x1, x2, slot_ref, out, held, sent, slot_v, row_v, row_s, sems, out_sems, row_sems):
         to_vmem = pltpu.make_async_copy(slot_ref, slot_v, row_sems.at[0])
         to_vmem.start()
         copies = []
@@ -72,22 +75,25 @@
         row_v[...] = slot_rows(slot_v[...], segments, span)
         to_smem = pltpu.make_async_copy(row_v, row_s, row_sems.at[1])
         to_smem.start()
-        mark[...] = jnp.zeros_like(mark)
         to_smem.wait()
         for c in copies:
             c.wait()
 
+        here = side_ref[0]
+
         def peer(j, carry):
+            start = j * both + 1 - here
             for q in range(per_peer):
                 row = row_s[0, j * per_peer + q]
-                sent[pl.ds(j * 2 * message + q, 6, stride=per_peer), :] = held[
-                    pl.ds(row, 6, stride=span), :
-                ]
+                sent[pl.ds(start + q, 6, stride=per_peer), :] = held[pl.ds(row, 6, stride=span), :]
             return carry
 
         leaving = []
         for n in range(devices // at_once):
             lax.fori_loop(n * at_once, (n + 1) * at_once, peer, 0)
+            last = n * part + both - 2
+            moved = sent[pl.ds(last - here * (message - 1), at_once, stride=both), :]
+            sent[pl.ds(last, at_once, stride=both), :] = moved
             rows = pl.ds(n * part, part)
             leaving.append(pltpu.make_async_copy(sent.at[rows], out.at[rows], out_sems.at[n]))
             leaving[-1].start()
@@ -96,17 +102,15 @@
 
     hbm = pl.BlockSpec(memory_space=pltpu.HBM)
     vmem = pl.BlockSpec(memory_space=pltpu.VMEM)
+    smem = pl.BlockSpec(memory_space=pltpu.SMEM)
     return pl.pallas_call(
         kernel,
-        out_shape=(
-            pltpu.HBM((6 * blocks, SEGW), jnp.float32),
-            jax.ShapeDtypeStruct((SUB, SEGW), jnp.float32),
-        ),
-        in_specs=[hbm, hbm, hbm, hbm],
-        out_specs=(hbm, vmem),
+        out_shape=pltpu.HBM((devices * both, SEGW), jnp.float32),
+        in_specs=[smem, hbm, hbm, hbm, hbm],
+        out_specs=hbm,
         scratch_shapes=[
             pltpu.VMEM((6 * groups * span, SEGW), jnp.float32),
-            pltpu.VMEM((6 * blocks, SEGW), jnp.float32),
+            pltpu.VMEM((devices * both, SEGW), jnp.float32),
             pltpu.VMEM((1, blocks), jnp.int32),
             pltpu.VMEM((1, blocks), jnp.int32),
             pltpu.SMEM((1, blocks), jnp.int32),
@@ -116,19 +120,51 @@
         ],
         compiler_params=pltpu.CompilerParams(vmem_limit_bytes=20 << 20),
         name="pack",
-    )(*(in_hbm(x) for x in xs), in_hbm(slots))
-
-
-def unpack_step(arrived, first_rows, scaled, devices, per_peer, segments):
-    groups, _, half_rows, _ = scaled.shape
+    )(side, *(in_hbm(x) for x in xs), in_hbm(slots))
+
+
+def stamp(packed, side, sums, devices):
+    both = packed.shape[0] // devices
+    last = both - 1
+
+    def kernel(side_ref, one_ref, two_ref, packed_ref, out, row, sems):
+        row[...] = jnp.broadcast_to(one_ref[...] + two_ref[...], row.shape)
+        copies = [
+            pltpu.make_async_copy(row, out.at[:, side_ref[0] * (both // 2 - 1)], sems.at[0]),
+            pltpu.make_async_copy(row, out.at[:, last], sems.at[1]),
+        ]
+        for c in copies:
+            c.start()
+        for c in copies:
+            c.wait()
+
+    smem = pl.BlockSpec(memory_space=pltpu.SMEM)
+    vmem = pl.BlockSpec(memory_space=pltpu.VMEM)
+    hbm = pl.BlockSpec(memory_space=pltpu.HBM)
+    shape = (devices, both, 1, SEGW)
+    return pl.pallas_call(
+        kernel,
+        out_shape=pltpu.HBM(shape, jnp.float32),
+        in_specs=[smem, vmem, vmem, hbm],
+        out_specs=hbm,
+        input_output_aliases={3: 0},
+        scratch_shapes=[pltpu.VMEM((devices, 1, SEGW), jnp.float32), pltpu.SemaphoreType.DMA((2,))],
+        compiler_params=pltpu.CompilerParams(vmem_limit_bytes=4 << 20),
+        name="stamp",
+    )(side, *sums, in_hbm(packed.reshape(shape)))
+
+
+def unpack_step(arrived, first_rows, wide, side, limit, devices, per_peer, segments):
+    groups, _, half_rows, _ = wide.shape
     span = half_rows + PAD
     blocks = devices * per_peer
-    message = 3 * per_peer
+    message = 3 * per_peer + 1
+    both = 2 * message
     tile = 4 * SUB
     at_once = 8
-    part = at_once * 2 * message
-
-    def kernel(in_ref, row_ref, grad_ref, o0, o1, o2, held, came, row_s, sems, in_sems, row_sem):
+    part = at_once * both
+
+    def kernel(side_ref, in_ref, row_ref, grad_ref, o0, o1, o2, held, came, row_s, sems, in_sems, row_sem):
         to_smem = pltpu.make_async_copy(row_ref, row_s, row_sem)
         to_smem.start()
         coming = []
@@ -137,18 +173,24 @@
             coming.append(pltpu.make_async_copy(in_ref.at[rows], came.at[rows], in_sems.at[n]))
             coming[-1].start()
         to_smem.wait()
+        here = side_ref[0]
 
         def peer(i, carry):
+            start = i * both + 1 - here
             for q in range(per_peer):
                 row = row_s[0, i * per_peer + q]
-                held[pl.ds(row, 6, stride=span), :] = came[
-                    pl.ds(i * 2 * message + q, 6, stride=per_peer), :
-                ]
+                held[pl.ds(row, 6, stride=span), :] = came[pl.ds(start + q, 6, stride=per_peer), :]
             return carry
 
+        sums = jnp.zeros((at_once, SEGW), jnp.float32)
         for n in range(devices // at_once):
             coming[n].wait()
+            first = pl.ds(n * part + here * (message - 1), at_once, stride=both)
+            sums += came[first, :] + came[pl.ds(n * part + both - 1, at_once, stride=both), :]
+            came[first, :] = came[pl.ds(n * part + both - 2, at_once, stride=both), :]
             lax.fori_loop(n * at_once, (n + 1) * at_once, peer, 0)
+        sum_squares = jnp.sum(sums, axis=0, keepdims=True)
+        clip_scale = jnp.minimum(1.0, limit / jnp.sqrt(sum_squares + 1e-06))
         copies = []
         for g in range(groups):
             for k in range(2):
@@ -159,7 +201,7 @@
                         start = pl.multiple_of(at + a * span + n * tile, SUB)
                         return pl.ds(start, tile)
 
-                    scaled_here = grad_ref[g, k, pl.ds(pl.multiple_of(n * tile, SUB), tile), :]
+                    scaled_here = clip_scale * grad_ref[g, k, pl.ds(pl.multiple_of(n * tile, SUB), tile), :]
                     old = held[rows(0), :]
                     moment1 = beta_one * held[rows(1), :] + (1.0 - beta_one) * scaled_here
                     moment2 = beta_two * held[rows(2), :] + (1.0 - beta_two) * scaled_here * scaled_here
@@ -182,15 +224,16 @@
 
     hbm = pl.BlockSpec(memory_space=pltpu.HBM)
     vmem = pl.BlockSpec(memory_space=pltpu.VMEM)
-    out = pltpu.HBM(scaled.shape, jnp.float32)
+    smem = pl.BlockSpec(memory_space=pltpu.SMEM)
+    out = pltpu.HBM(wide.shape, jnp.float32)
     return pl.pallas_call(
         kernel,
         out_shape=(out, out, out),
-        in_specs=[hbm, hbm, vmem],
+        in_specs=[smem, hbm, hbm, vmem],
         out_specs=(hbm, hbm, hbm),
         scratch_shapes=[
             pltpu.VMEM((6 * groups * span, SEGW), jnp.float32),
-            pltpu.VMEM((6 * blocks, SEGW), jnp.float32),
+            pltpu.VMEM((devices * both, SEGW), jnp.float32),
             pltpu.SMEM((1, blocks), jnp.int32),
             pltpu.SemaphoreType.DMA((6 * groups,)),
             pltpu.SemaphoreType.DMA((devices // at_once,)),
@@ -198,18 +241,7 @@
         ],
         compiler_params=pltpu.CompilerParams(vmem_limit_bytes=20 << 20),
         name="unpack_step",
-    )(in_hbm(arrived), in_hbm(first_rows), scaled)
-
-
-def sum_over(value, axes):
-    for axis in axes:
-        count = lax.axis_size(axis)
-        apart = 1
-        while apart < count:
-            route = [(n, n ^ apart) for n in range(count)]
-            value = value + lax.ppermute(value, axis, route)
-            apart *= 2
-    return value
+    )(side, in_hbm(arrived), in_hbm(first_rows), wide)
 
 
 def per_device(total, master_old, moment1_old, moment2_old, grad, send_slots, recv_slots):
@@ -219,19 +251,22 @@
     devices = lax.axis_size(DP)
     per_peer = rows * segments // devices
     xs = [tiled(x, groups, half_rows) for x in (master_old, moment1_old, moment2_old)]
-    packed, mark = pack(xs, send_slots, devices, per_peer, segments)
-    outgoing = packed.reshape(2 * devices, 3 * per_peer, 1, SEGW)
+    side = lax.axis_index("side").astype(jnp.int32).reshape(1)
+
+    wide = grad.astype(jnp.float32)
+    own_sum = jnp.sum(wide * wide).reshape(1, 1)
+    other_sum = lax.ppermute(own_sum, "pair", [(0, 1), (1, 0)])
+    packed = pack(xs, send_slots, side, devices, per_peer, segments)
+    outgoing = stamp(packed, side, (own_sum, other_sum), devices)
+    outgoing = outgoing.reshape(2 * devices, 3 * per_peer + 1, 1, SEGW)
     arrived = lax.all_to_all(outgoing, DP_SIDE, split_axis=0, concat_axis=0, tiled=True)
-    arrived = arrived.reshape(6 * devices * per_peer, SEGW)
-
-    grad, recv_slots, mark = lax.optimization_barrier((grad, recv_slots, mark))
+    arrived = arrived.reshape(packed.shape)
+
     first_rows = slot_rows(recv_slots, segments, half_rows + PAD)
-    wide = grad.astype(jnp.float32)
-    sum_squares = sum_over(jnp.sum(wide * wide).reshape(1, 1), DP_TENSOR)
-    limit = clip_ratio * jnp.sqrt(jnp.float32(total))
-    clip_scale = jnp.minimum(1.0, limit / jnp.sqrt(sum_squares + 1e-06))
-    scaled = tiled(clip_scale * wide, groups, half_rows)
-    outs = unpack_step(arrived, first_rows, scaled, devices, per_peer, segments)
+    limit = clip_ratio * math.sqrt(total)
+    outs = unpack_step(
+        arrived, first_rows, tiled(wide, groups, half_rows), side, limit, devices, per_peer, segments
+    )
     return tuple(untiled(o, rows, columns) for o in outs)
 
 

time: 183 us -> 159 us (0.87)
  starting transfers between devices: 43 us -> 17.6 us
  waiting for transfers between devices: 115 us -> 121 us
  between operations: 6.5 us -> 0.7 us
    all_to_all x1, waiting for transfers between devices: 0.01 us -> 121 us  [per_device(): lax.all_to_all(outgoing, DP_SIDE, split_axis=0, concat_axis=0, tiled=True)]
    ppermute x8 -> x1, waiting for transfers between devices: 115 us -> 0.01 us  [per_device(): other_sum = lax.ppermute(own_sum, 'pair', [(0, 1), (1, 0)])]
    ppermute x8 -> x1, starting transfers between devices: 27.7 us -> 3.73 us  [per_device(): other_sum = lax.ppermute(own_sum, 'pair', [(0, 1), (1, 0)])]
    pallas_call x2 -> x3, Pallas kernels: 14.5 us -> 16 us  [the longest x1 7.27 us: unpack_step(): pl.pallas_call(kernel, out_shape=(out, out, out), in_specs=[smem, hbm, hb...]
  transfers between devices with their start and end apart: 9 -> 2, of which waited for: 7 -> 1; matrix products, arithmetic and copies ran while one was open for 1% -> 0% of each run, Pallas kernels for 0% -> 4%
where the time goes in v2:
time: 159 us
  waiting for transfers between devices  121 us (76%)
  starting transfers between devices  17.6 us (11%)
  Pallas kernels  16 us (10%)
  other arithmetic  2.96 us (2%)
    all_to_all x1, waiting for transfers between devices, per_device(): lax.all_to_all(outgoing, DP_SIDE, split_axis=0, concat_axis=0, tiled=True)  121 us
    all_to_all x1, starting transfers between devices, per_device(): lax.all_to_all(outgoing, DP_SIDE, split_axis=0, concat_axis=0, tiled=True)  13.9 us
    pallas_call x1, Pallas kernels, unpack_step(): pl.pallas_call(kernel, out_shape=(out, out, out), in_specs=[smem, hbm, hb...  7.27 us
    pallas_call x1, Pallas kernels, pack(): pl.pallas_call(kernel, out_shape=pltpu.HBM((devices * both, SEGW), jnp.fl...  6.79 us
    ppermute x1, starting transfers between devices, per_device(): other_sum = lax.ppermute(own_sum, 'pair', [(0, 1), (1, 0)])  3.73 us
  transfers between devices with their start and end apart: 2, of which 1 were waited for; matrix products, arithmetic and copies ran while one was open for 0% of the time, Pallas kernels for 4%

profile of v2, /device:TPU:1, one launch (start us, length us, event | category | flops | bytes accessed | tf_op | source)
XLA Modules:
  0.0 158.6 jit_solution(11470210121997913750)
XLA Ops:
  0.6 2.2 %multiply_reduce_fusion = f32[]{:T(128)} fusion(bf16[48,9216]{1,0:T(8,128)(2,1)} %param.9), kind=kLoop, calls=%fused_computation | loop fusion | flops 1327103 | bytes 884740 | tf_op jit(solution)/shard_map/reduce_sum | solution.py:257
  2.9 3.7 %collective-permute-start = (f32[1,1]{1,0:T(1,128)}, f32[1,1]{1,0:T(1,128)}, u32[]{:S(2)}, u32[]{:S(2)}) collective-permute-start(f32[1,1]{1,0:T(1,128)} %bitcast.1.one_ref), channel_id=1, source_target_pairs={{0,2},{2,0},{1,3},{3,1},{4,6},{6,4},{5,7},{7,5},{8,10},{10,8},{9,1... | collective-permute-start | bytes 20 | tf_op jit(solution)/shard_map/ppermute | solution.py:258
  6.6 6.8 %pack.1 = f32[10496,128]{1,0:T(8,128)} custom-call(s32[1]{0:T(128)} %bitcast.side_ref, f32[6,2,288,128]{3,2,1,0:T(8,128)} %bitcast.43, f32[6,2,288,128]{3,2,1,0:T(8,128)} %bitcast.44, f32[6,2,288,128]{3,2,1,0:T(8,128)} %bitcast.45, s32[1,1728]{1,0:T(1,128)} %slot_ref.1), custom_call_target="tpu_custom_call" | custom-call | tf_op jit(solution)/shard_map/pack/pallas_call | solution.py:106
  13.4 0.0 collective-permute-done.two_ref
  13.4 2.0 %stamp.1 = f32[64,164,1,128]{3,2,1,0:T(1,128)} custom-call(s32[1]{0:T(128)} %bitcast.side_ref, f32[1,1]{1,0:T(1,128)} %bitcast.1.one_ref, f32[1,1]{1,0:T(1,128)} %collective-permute-done.two_ref, f32[64,164,1,128]{3,2,1,0:T(1,128)} %bitcast.41), custom_call_target="tpu_custom_call", output_to_operand_aliasing={{}: (3, {})} | custom-call | tf_op jit(solution)/shard_map/stamp/pallas_call | solution.py:145
  15.4 0.0 copy-start
  15.4 13.9 %all-to-all-start = ((f32[128,82,1,128]{3,2,1,0:T(1,128)}), f32[128,82,1,128]{3,2,1,0:T(1,128)}, u32[]{:S(2)}, u32[]{:S(2)}) async-start(f32[128,82,1,128]{3,2,1,0:T(1,128)} %bitcast.42), calls=%async_computation | async-start | bytes 10747904 | tf_op jit(solution)/shard_map/all_to_all | solution.py:262
  29.3 0.0 copy-done
  29.3 0.0 copy-start.1
  29.3 0.1 convert_element_type.3
  29.4 0.6 copy-done.1
  30.0 0.6 and_add_fusion.row_ref
  30.6 120.7 %all-to-all-done = f32[128,82,1,128]{3,2,1,0:T(1,128)} async-done(((f32[128,82,1,128]{3,2,1,0:T(1,128)}), f32[128,82,1,128]{3,2,1,0:T(1,128)}, u32[]{:S(2)}, u32[]{:S(2)}) %all-to-all-start) | async-done | bytes 5373984 | tf_op jit(solution)/shard_map/all_to_all | solution.py:262
  151.3 7.3 %unpack_step.1 = (f32[6,2,288,128]{3,2,1,0:T(8,128)}, f32[6,2,288,128]{3,2,1,0:T(8,128)}, f32[6,2,288,128]{3,2,1,0:T(8,128)}) custom-call(s32[1]{0:T(128)} %bitcast.side_ref, f32[10496,128]{1,0:T(8,128)} %bitcast.13.in_ref, s32[1,1728]{1,0:T(1,128)} %and_add_fusion.row_ref, f32[6,2,288,128]{3,2,1,0:T(8,128)S(1)} %bitcast.40), custom_call_target="tpu_custom_call" | custom-call | tf_op jit(solution)/shard_map/unpack_step/pallas_call | solution.py:229
Async XLA Ops:
  2.9 10.5 %collective-permute-start = (f32[1,1]{1,0:T(1,128)}, f32[1,1]{1,0:T(1,128)}, u32[]{:S(2)}, u32[]{:S(2)}) collective-permute-start(f32[1,1]{1,0:T(1,128)} %bitcast.1.one_ref), channel_id=1, source_target_pairs={{0,2},{2,0},{1,3},{3,1},{4,6},{6,4},{5,7},{7,5},{8,10},{10,8},{9,1... | collective-permute-start | bytes 20 | tf_op jit(solution)/shard_map/ppermute | solution.py:258
  15.4 13.9 %copy-start = (bf16[48,9216]{1,0:T(8,128)(2,1)S(1)}, bf16[48,9216]{1,0:T(8,128)(2,1)}, u32[]{:S(2)}) copy-start(bf16[48,9216]{1,0:T(8,128)(2,1)} %param.9) | copy-start | bytes 2654212
  15.4 136.0 %all-to-all-start = ((f32[128,82,1,128]{3,2,1,0:T(1,128)}), f32[128,82,1,128]{3,2,1,0:T(1,128)}, u32[]{:S(2)}, u32[]{:S(2)}) async-start(f32[128,82,1,128]{3,2,1,0:T(1,128)} %bitcast.42), calls=%async_computation | async-start | bytes 10747904 | tf_op jit(solution)/shard_map/all_to_all | solution.py:262
  29.3 0.7 copy-start.1

commit v3 on v2

v3 whole, which is shorter than its diff:
```python
import math

import jax
import jax.numpy as jnp
from jax import lax
from jax.experimental import pallas as pl
from jax.experimental.pallas import tpu as pltpu
from jax.sharding import Mesh
from jax.sharding import PartitionSpec as P

SEGW = 128
SUB = 8
DP = ("dp_0", "dp_1", "dp_2")
DP_TENSOR = ("dp_0", "dp_1", "dp_2", "pair", "side")
DP_SIDE = ("dp_0", "dp_1", "dp_2", "side")
PAD = 8

beta_one = 0.9
beta_two = 0.95
correct_one = 0.6513215599
correct_two = 0.4012630608
adam_eps = 1e-08
learning_rate = 0.01
weight_decay = 0.1
clip_ratio = 0.75


def tiled(x, groups, half_rows):
    rows, columns = x.shape
    tiles = x.reshape(groups, SUB, columns // SEGW, SEGW).transpose(0, 2, 1, 3)
    return tiles.reshape(groups, 2, half_rows, SEGW)


def untiled(x, rows, columns):
    groups = rows // SUB
    tiles = x.reshape(groups, columns // SEGW, SUB, SEGW).transpose(0, 2, 1, 3)
    return tiles.reshape(rows, columns)


def in_vmem(x):
    return pltpu.with_memory_space_constraint(x, pltpu.VMEM)


def in_hbm(x):
    return pltpu.with_memory_space_constraint(x, pltpu.HBM)


def slot_rows(slots, segments, span):
    r = lax.shift_right_logical(slots * (-(-65536 // segments)), 16)
    s = slots - r * segments
    return lax.shift_right_logical(r, 3) * (6 * span) + s * SUB + (r & (SUB - 1))


def pack(xs, slots, new_slots, side, devices, per_peer, segments):
    groups, _, half_rows, _ = xs[0].shape
    span = half_rows + PAD
    blocks = devices * per_peer
    message = 3 * per_peer + 1
    both = 2 * message

    def kernel(side_ref, x0, x1, x2, slot_ref, new_ref, sent, new_rows, held, slot_v, new_v, row_v, row_s, sems, row_sems):
        to_vmem = pltpu.make_async_copy(slot_ref, slot_v, row_sems.at[0])
        to_vmem.start()
        new_to_vmem = pltpu.make_async_copy(new_ref, new_v, row_sems.at[2])
        new_to_vmem.start()
        copies = []
        for g in range(groups):
            for k in range(2):
                for a, x in enumerate((x0, x1, x2)):
                    at = 6 * g + 3 * k + a
                    copies.append(
                        pltpu.make_async_copy(
                            x.at[g, k], held.at[pl.ds(at * span, half_rows)], sems.at[at]
                        )
                    )
        for c in copies:
            c.start()
        to_vmem.wait()
        row_v[...] = slot_rows(slot_v[...], segments, span)
        to_smem = pltpu.make_async_copy(row_v, row_s, row_sems.at[1])
        to_smem.start()
        new_to_vmem.wait()
        new_rows[...] = slot_rows(new_v[...], segments, span)
        to_smem.wait()
        for c in copies:
            c.wait()

        here = side_ref[0]

        def peer(j, carry):
            start = j * both + 1 - here
            for q in range(per_peer):
                row = row_s[0, j * per_peer + q]
                sent[pl.ds(start + q, 6, stride=per_peer), :] = held[pl.ds(row, 6, stride=span), :]
            return carry

        lax.fori_loop(0, devices, peer, 0)
        for n in range(devices // SUB):
            last = n * SUB * both + both - 2
            moved = sent[pl.ds(last - here * (message - 1), SUB, stride=both), :]
            sent[pl.ds(last, SUB, stride=both), :] = moved

    hbm = pl.BlockSpec(memory_space=pltpu.HBM)
    vmem = pl.BlockSpec(memory_space=pltpu.VMEM)
    smem = pl.BlockSpec(memory_space=pltpu.SMEM)
    return pl.pallas_call(
        kernel,
        out_shape=(
            pltpu.VMEM((devices * both, SEGW), jnp.float32),
            jax.ShapeDtypeStruct((1, blocks), jnp.int32),
        ),
        in_specs=[smem, hbm, hbm, hbm, hbm, hbm],
        out_specs=(vmem, vmem),
        scratch_shapes=[
            pltpu.VMEM((6 * groups * span, SEGW), jnp.float32),
            pltpu.VMEM((1, blocks), jnp.int32),
            pltpu.VMEM((1, blocks), jnp.int32),
            pltpu.VMEM((1, blocks), jnp.int32),
            pltpu.SMEM((1, blocks), jnp.int32),
            pltpu.SemaphoreType.DMA((6 * groups,)),
            pltpu.SemaphoreType.DMA((3,)),
        ],
        compiler_params=pltpu.CompilerParams(vmem_limit_bytes=20 << 20),
        name="pack",
    )(side, *(in_hbm(x) for x in xs), in_hbm(slots), in_hbm(new_slots))


def stamp(packed, side, sums, devices):
    both = packed.shape[0] // devices

    def kernel(side_ref, one_ref, two_ref, packed_ref, out):
        row = jnp.broadcast_to(one_ref[...] + two_ref[...], (SUB, SEGW))
        for n in range(devices // SUB):
            start = n * SUB * both
            out[pl.ds(start + side_ref[0] * (both // 2 - 1), SUB, stride=both), :] = row
            out[pl.ds(start + both - 1, SUB, stride=both), :] = row

    smem = pl.BlockSpec(memory_space=pltpu.SMEM)
    vmem = pl.BlockSpec(memory_space=pltpu.VMEM)
    return pl.pallas_call(
        kernel,
        out_shape=pltpu.VMEM(packed.shape, jnp.float32),
        in_specs=[smem, vmem, vmem, vmem],
        out_specs=vmem,
        input_output_aliases={3: 0},
        compiler_params=pltpu.CompilerParams(vmem_limit_bytes=16 << 20),
        name="stamp",
    )(side, *sums, in_vmem(packed))


def unpack_step(arrived, first_rows, grad, side, limit, devices, per_peer, segments):
    groups, _, half_rows, _ = grad.shape
    span = half_rows + PAD
    blocks = devices * per_peer
    message = 3 * per_peer + 1
    both = 2 * message
    tile = 4 * SUB

    def kernel(side_ref, came, row_ref, grad_ref, o0, o1, o2, held, row_s, sems, row_sem):
        to_smem = pltpu.make_async_copy(row_ref, row_s, row_sem)
        to_smem.start()
        here = side_ref[0]
        sums = jnp.zeros((SUB, SEGW), jnp.float32)
        for n in range(devices // SUB):
            first = n * SUB * both
            sums += came[pl.ds(first + here * (message - 1), SUB, stride=both), :]
            sums += came[pl.ds(first + both - 1, SUB, stride=both), :]
        sum_squares = jnp.sum(sums, axis=0, keepdims=True)
        clip_scale = jnp.minimum(1.0, limit / jnp.sqrt(sum_squares + 1e-06))
        to_smem.wait()

        def peer(i, carry):
            start = i * both + 1 - here
            for q in range(per_peer):
                row = row_s[0, i * per_peer + q]
                held[pl.ds(row, 6, stride=span), :] = came[pl.ds(start + q, 6, stride=per_peer), :]
            row = row_s[0, i * per_peer] + 3 * span
            held[pl.ds(row, 1), :] = came[pl.ds(i * both + message + here * (message - 2), 1), :]
            return carry

        lax.fori_loop(0, devices, peer, 0)
        copies = []
        for g in range(groups):
            for k in range(2):
                at = (6 * g + 3 * k) * span

                def update(n, carry, at=at, g=g, k=k):
                    def rows(a):
                        start = pl.multiple_of(at + a * span + n * tile, SUB)
                        return pl.ds(start, tile)

                    scaled_here = clip_scale * grad_ref[
                        g, k, pl.ds(pl.multiple_of(n * tile, SUB), tile), :
                    ].astype(jnp.float32)
                    old = held[rows(0), :]
                    moment1 = beta_one * held[rows(1), :] + (1.0 - beta_one) * scaled_here
                    moment2 = beta_two * held[rows(2), :] + (1.0 - beta_two) * scaled_here * scaled_here
                    step = moment1 / correct_one / (jnp.sqrt(moment2 / correct_two) + adam_eps)
                    held[rows(0), :] = old - learning_rate * (step + weight_decay * old)
                    held[rows(1), :] = moment1
                    held[rows(2), :] = moment2
                    return carry

                lax.fori_loop(0, half_rows // tile, update, 0)
                for a, o in enumerate((o0, o1, o2)):
                    copies.append(
                        pltpu.make_async_copy(
                            held.at[pl.ds(at + a * span, half_rows)], o.at[g, k], sems.at[6 * g + 3 * k + a]
                        )
                    )
                    copies[-1].start()
        for c in copies:
            c.wait()

    hbm = pl.BlockSpec(memory_space=pltpu.HBM)
    vmem = pl.BlockSpec(memory_space=pltpu.VMEM)
    smem = pl.BlockSpec(memory_space=pltpu.SMEM)
    out = pltpu.HBM(grad.shape, jnp.float32)
    return pl.pallas_call(
        kernel,
        out_shape=(out, out, out),
        in_specs=[smem, vmem, hbm, vmem],
        out_specs=(hbm, hbm, hbm),
        scratch_shapes=[
            pltpu.VMEM((6 * groups * span, SEGW), jnp.float32),
            pltpu.SMEM((1, blocks), jnp.int32),
            pltpu.SemaphoreType.DMA((6 * groups,)),
            pltpu.SemaphoreType.DMA,
        ],
        compiler_params=pltpu.CompilerParams(vmem_limit_bytes=20 << 20),
        name="unpack_step",
    )(side, in_vmem(arrived), in_hbm(first_rows), grad)


def per_device(total, master_old, moment1_old, moment2_old, grad, send_slots, recv_slots):
    rows, columns = master_old.shape
    segments = columns // 2 // SEGW
    groups, half_rows = rows // SUB, SUB * segments
    devices = lax.axis_size(DP)
    per_peer = rows * segments // devices
    xs = [tiled(x, groups, half_rows) for x in (master_old, moment1_old, moment2_old)]
    side = lax.axis_index("side").astype(jnp.int32).reshape(1)

    wide = grad.astype(jnp.float32)
    own_sum = jnp.sum(wide * wide).reshape(1, 1)
    other_sum = lax.ppermute(own_sum, "pair", [(0, 1), (1, 0)])
    packed, first_rows = pack(xs, send_slots, recv_slots, side, devices, per_peer, segments)
    outgoing = stamp(packed, side, (own_sum, other_sum), devices)
    outgoing = outgoing.reshape(2 * devices, 3 * per_peer + 1, 1, SEGW)
    arrived = lax.all_to_all(outgoing, DP_SIDE, split_axis=0, concat_axis=0, tiled=True)
    arrived = arrived.reshape(packed.shape)

    limit = clip_ratio * math.sqrt(total)
    outs = unpack_step(
        arrived, first_rows, tiled(grad, groups, half_rows), side, limit, devices, per_peer, segments
    )
    return tuple(untiled(o, rows, columns) for o in outs)


def solution(mesh):
    split = Mesh(mesh.devices.reshape(8, 4, 2, mesh.shape["tensor"] // 2, 2), DP_TENSOR)
    wide_spec = P(DP, ("pair", "side"))

    def whole(master_old, *rest):
        def body(*args):
            return per_device(master_old.size, *args)

        return jax.shard_map(
            body,
            mesh=split,
            in_specs=(wide_spec,) * 4 + (P(DP, None),) * 2,
            out_specs=(wide_spec,) * 3,
            check_vma=False,
        )(master_old, *rest)

    return whole
```

time: 159 us -> 156 us (0.981)
  blocking collectives: 0 us -> 135 us
  waiting for transfers between devices: 121 us -> 0.01 us
  starting transfers between devices: 17.6 us -> 3.73 us
  Pallas kernels: 16 us -> 14.2 us
    all_to_all x0 -> x1, blocking collectives: none -> 135 us  [per_device(): lax.all_to_all(outgoing, DP_SIDE, split_axis=0, concat_axis=0, tiled=True)]
    all_to_all x1 -> x0, waiting for transfers between devices: 121 us -> none  [per_device(): lax.all_to_all(outgoing, DP_SIDE, split_axis=0, concat_axis=0, tiled=True)]
    all_to_all x1 -> x0, starting transfers between devices: 13.9 us -> none  [per_device(): lax.all_to_all(outgoing, DP_SIDE, split_axis=0, concat_axis=0, tiled=True)]
    pallas_call x3, Pallas kernels: 16 us -> 14.2 us  [the longest x1 7.02 us: unpack_step(): pl.pallas_call(kernel, out_shape=(out, out, out), in_specs=[smem, vmem, h...]
  transfers between devices with their start and end apart: 2 -> 1, of which waited for: 1 -> 0; matrix products, arithmetic and copies ran while one was open for 0% -> 0% of each run, Pallas kernels for 4% -> 4%
where the time goes in v3:
time: 156 us
  blocking collectives  135 us (87%)
  Pallas kernels  14.2 us (9%)
  starting transfers between devices  3.73 us (2%)
  other arithmetic  2.23 us (1%)
    all_to_all x1, blocking collectives, per_device(): lax.all_to_all(outgoing, DP_SIDE, split_axis=0, concat_axis=0, tiled=True)  135 us
    pallas_call x1, Pallas kernels, unpack_step(): pl.pallas_call(kernel, out_shape=(out, out, out), in_specs=[smem, vmem, h...  7.02 us
    pallas_call x1, Pallas kernels, pack(): pl.pallas_call(kernel, out_shape=(pltpu.VMEM((devices * both, SEGW), jnp....  5.82 us
    ppermute x1, starting transfers between devices, per_device(): other_sum = lax.ppermute(own_sum, 'pair', [(0, 1), (1, 0)])  3.73 us
  transfers between devices with their start and end apart: 1, of which 0 were waited for; matrix products, arithmetic and copies ran while one was open for 0% of the time, Pallas kernels for 4%

profile of v3, /device:TPU:1, one launch (start us, length us, event | category | flops | bytes accessed | tf_op | source)
XLA Modules:
  0.0 155.8 jit_solution(6674533525202861401)
XLA Ops:
  0.6 2.2 %multiply_reduce_fusion = f32[]{:T(128)} fusion(bf16[48,9216]{1,0:T(8,128)(2,1)} %param.9), kind=kLoop, calls=%fused_computation | loop fusion | flops 1327103 | bytes 884740 | tf_op jit(solution)/shard_map/reduce_sum | solution.py:245
  2.9 3.7 %collective-permute-start = (f32[1,1]{1,0:T(1,128)}, f32[1,1]{1,0:T(1,128)}, u32[]{:S(2)}, u32[]{:S(2)}) collective-permute-start(f32[1,1]{1,0:T(1,128)} %bitcast.1.one_ref), channel_id=1, source_target_pairs={{0,2},{2,0},{1,3},{3,1},{4,6},{6,4},{5,7},{7,5},{8,10},{10,8},{9,1... | collective-permute-start | bytes 20 | tf_op jit(solution)/shard_map/ppermute | solution.py:246
  6.6 5.8 %pack.1 = (f32[10496,128]{1,0:T(8,128)S(1)}, s32[1,1728]{1,0:T(1,128)S(1)}) custom-call(s32[1]{0:T(128)} %bitcast.side_ref, f32[6,2,288,128]{3,2,1,0:T(8,128)} %bitcast.42, f32[6,2,288,128]{3,2,1,0:T(8,128)} %bitcast.43, f32[6,2,288,128]{3,2,1,0:T(8,128)} %bitcast.44, s32[1,1728]{1,0:T(1,128)} %slot_ref.1, s32[1,1728]{1,0:T(1,128)} %new_ref.1), custom_call_target="tpu_custom_call" | custom-call | tf_op jit(solution)/shard_map/pack/pallas_call | solution.py:106
  12.4 0.0 copy-start.1
  12.4 0.0 collective-permute-done.two_ref
  12.4 1.3 stamp.1
  13.8 0.0 copy-done.1
  13.8 0.0 copy-start
  13.8 135.0 %all_to_all.5 = f32[128,82,1,128]{3,2,1,0:T(1,128)S(1)} all-to-all(f32[128,82,1,128]{3,2,1,0:T(1,128)S(1)} %bitcast.39), channel_id=1, replica_groups=mesh['dp_0'=8,'dp_1'=4,'dp_2'=2,'pair'=2,'side'=2] {'dp_0','dp_1','dp_2'..., dimensions={0} | all-to-all | bytes 10747904 | tf_op jit(solution)/shard_map/all_to_all | solution.py:250
  148.8 0.0 copy-done
  148.8 7.0 %unpack_step.1 = (f32[6,2,288,128]{3,2,1,0:T(8,128)}, f32[6,2,288,128]{3,2,1,0:T(8,128)}, f32[6,2,288,128]{3,2,1,0:T(8,128)}) custom-call(s32[1]{0:T(128)} %bitcast.side_ref, f32[10496,128]{1,0:T(8,128)S(1)} %bitcast.40, s32[1,1728]{1,0:T(1,128)} %copy-done.1, bf16[6,2,288,128]{3,2,1,0:T(8,128)(2,1)S(1)} %bitcast.41), custom_call_target="tpu_custom_call" | custom-call | tf_op jit(solution)/shard_map/unpack_step/pallas_call | solution.py:219
Async XLA Ops:
  2.9 9.6 %collective-permute-start = (f32[1,1]{1,0:T(1,128)}, f32[1,1]{1,0:T(1,128)}, u32[]{:S(2)}, u32[]{:S(2)}) collective-permute-start(f32[1,1]{1,0:T(1,128)} %bitcast.1.one_ref), channel_id=1, source_target_pairs={{0,2},{2,0},{1,3},{3,1},{4,6},{6,4},{5,7},{7,5},{8,10},{10,8},{9,1... | collective-permute-start | bytes 20 | tf_op jit(solution)/shard_map/ppermute | solution.py:246
  12.4 1.4 copy-start.1
  13.8 135.0 %copy-start = (bf16[48,9216]{1,0:T(8,128)(2,1)S(1)}, bf16[48,9216]{1,0:T(8,128)(2,1)}, u32[]{:S(2)}) copy-start(bf16[48,9216]{1,0:T(8,128)(2,1)} %param.9) | copy-start | bytes 2654212
